TPU v7x, 128 devices: a whole 4x4x4 slice. The times are simulated.
128 devices in a mesh: gx: 32 (over x, y, core), gy: 4 (over z).
Axes of the slice: x: 4, y: 4, z: 4, core: 2. Of those that a mesh axis runs over, the one named last changes fastest.
Arguments:
- signals: float32 [64, 32, 16, 128], P('gx', 'gy'), may hold values from -6 to 6
- tiles: bfloat16 [64, 32, 4, 128, 128], P('gx', 'gy'), may hold values from 0 to 0.00390625
- tile_dir: int32 [64, 32, 4], P('gx', 'gy'), may hold values from 0 to 8
- tile_mask: int32 [64, 32, 4], P('gx', 'gy'), may hold values 0 or 1
- live_rows: int32 [64, 32], P('gx', 'gy'), may hold values from 32 to 128
- bound_rows: int32 [64, 32], P('gx', 'gy'), may hold values from 1 to 32, as said below
- scale_coeffs: float32 [6, 5], replicated, may hold values from -1 to 1
- spectral_bound: float32 [1], replicated, may hold values from 2.5 to 4
Outputs:
- coefficients: float32 [6, 64, 32, 16, 128], P(None, 'gx', 'gy')
- energy: float32 [6, 16], replicated
Inputs may be any that keep to these rules, and one draw needn't show every extreme that they name: `bound_rows`: in every draw, some blocks on every device have exactly 32 boundary rows.
All inputs are finite; a program needn't handle non-finite values. No bound on the sum of `tile_mask` on one device may be relied on, other than what follows from the above.
Results may differ from a plain program's by a relative error of at most 0.0003.
Values may be sent and summed in bfloat16 or wider, within the bound.
No kernel may reach another device: no remote copies, remote signals or barrier semaphores. Data moves between devices by JAX's collectives and lax.ppermute only.
A program may use at most 64 MiB of HBM per device.

v0:
```python
import jax
import jax.numpy as jnp
from jax import lax
from jax.sharding import Mesh
from jax.sharding import PartitionSpec as P

DEG = 4
GX_GY = ("gx_0", "gx_1", "gx_2", "gy")
GX = ("gx_0", "gx_1", "gx_2")


def with_halo(array, sides, width):
    for axis, dim in sides:
        devices, length = (lax.axis_size(axis), array.shape[dim])
        up = [(i, (i + 1) % devices) for i in range(devices - 1)]
        down = [(j, i) for i, j in up]
        last = lax.slice_in_dim(array, length - width, length, axis=dim)
        first = lax.slice_in_dim(array, 0, width, axis=dim)
        before = lax.ppermute(last, axis, up)
        after = lax.ppermute(first, axis, down)
        array = jnp.concatenate([before, array, after], axis=dim)
    return array


def over_axes(array, axes):
    for axis in axes:
        array = lax.psum(array, axis)
    return array


def scaled_laplacian(values, adjacent, degree, factor):
    return factor * (degree * values - adjacent) - values


def shards(
    signals, tiles, tile_dir, tile_mask, live_rows, bound_rows, scale_coeffs, spectral_bound
):
    tile_size = signals.shape[3]
    extent_x = signals.shape[0]
    extent_y = signals.shape[1]
    slot_count = tiles.shape[2]
    block_count = extent_x * extent_y
    positions = lax.broadcasted_iota(jnp.int32, (1, 1, tile_size), 2)
    live_ind = (positions < live_rows[:, :, None]).astype(jnp.float32)
    bound_ind = (positions < bound_rows[:, :, None]).astype(jnp.float32)
    flat_tiles = tiles.reshape(block_count, slot_count, tile_size, tile_size)

    def adjacency(values):
        own_rows = values.astype(jnp.bfloat16)
        edge_rows = (values * bound_ind[:, :, None, :]).astype(jnp.bfloat16)
        padded = with_halo(edge_rows, ((GX, 0), ("gy", 1)), 1)
        slot_list = []
        for slot_index in range(slot_count):
            picked = jnp.zeros_like(own_rows)
            for direction in range(9):
                step_x = direction // 3 - 1
                step_y = direction % 3 - 1
                if direction == 4:
                    source = own_rows
                else:
                    source = padded[
                        1 + step_x : 1 + step_x + extent_x, 1 + step_y : 1 + step_y + extent_y
                    ]
                matches = (tile_dir[:, :, slot_index] == direction)[:, :, None, None]
                picked = jnp.where(matches, source, picked)
            kept = (tile_mask[:, :, slot_index] == 1)[:, :, None, None]
            picked = jnp.where(kept, picked, jnp.zeros_like(picked))
            slot_list.append(picked)
        inputs = jnp.stack(slot_list, axis=1 + 1)
        flat_inputs = inputs.reshape(block_count, slot_count, inputs.shape[3], tile_size)
        product = lax.dot_general(
            flat_inputs,
            flat_tiles,
            (((1, 3), (1, 3)), ((0,), (0,))),
            preferred_element_type=jnp.float32,
        )
        product = product.reshape(extent_x, extent_y, inputs.shape[3], tile_size)
        return product * live_ind[:, :, None, :]

    channels = signals.shape[2]
    initial = signals * live_ind[:, :, None, :]
    joined = jnp.concatenate([initial, live_ind[:, :, None, :]], axis=2)
    first_pass = adjacency(joined)
    degree = first_pass[:, :, channels:, :]
    factor = 2.0 / spectral_bound[0]
    previous = initial
    current = scaled_laplacian(initial, first_pass[:, :, :channels, :], degree, factor)
    totals = 0.5 * scale_coeffs[:, 0][:, None, None, None, None] * initial[None]
    totals = totals + scale_coeffs[:, 1][:, None, None, None, None] * current[None]
    for degree_index in range(2, DEG + 1):
        adjacent = adjacency(current)
        following = 2.0 * scaled_laplacian(current, adjacent, degree, factor) - previous
        previous = current
        current = following
        totals = totals + scale_coeffs[:, degree_index][:, None, None, None, None] * current[None]
    nodes = extent_x * extent_y * tile_size * lax.axis_size(GX) * lax.axis_size("gy")
    local_sums = jnp.sum(totals * totals, axis=(1, 2, 4))
    energy = over_axes(local_sums, GX_GY) / nodes
    return (totals, energy)


def solution(mesh):
    torus = Mesh(mesh.devices.reshape(4, 4, 2, mesh.shape["gy"]), ("gx_0", "gx_1", "gx_2", "gy"))
    placed = (
        P(GX, "gy", None, None),
        P(GX, "gy", None, None, None),
        P(GX, "gy", None),
        P(GX, "gy", None),
        P(GX, "gy"),
        P(GX, "gy"),
        P(),
        P(),
    )
    return jax.shard_map(
        shards,
        mesh=torus,
        in_specs=placed,
        out_specs=(P(None, GX, "gy", None, None), P()),
        check_vma=False,
    )
```

profile of v0, /device:TPU:8, one launch (start us, length us, event | category | flops | bytes accessed | tf_op | source)
XLA Modules:
  0.0 114.4 jit_solution(3090985521356103053)
XLA Ops:
  0.6 0.9 compare_convert_fusion
  1.6 0.8 fusion.35
  2.3 0.9 broadcast_multiply_fusion.1
  3.3 1.9 %collective-permute-start = (bf16[1,8,17,128]{3,2,1,0:T(8,128)(2,1)S(1)}, bf16[1,8,17,128]{3,2,1,0:T(8,128)(2,1)S(1)}, u32[]{:S(2)}, u32[]{:S(2)}) collective-permute-start(bf16[1,8,17,128]{3,2,1,0:T(8,128)(2,1)S(1)} %get-tuple-element.37), channel_id=1, source_target_pairs={{0,4},{4,8},{8,12},{12,16},{16,20},{20,24},{24,28},{28,32},{32,36}... | collective-permute-start | bytes 104456 | tf_op jit(solution)/shard_map/ppermute | solution.py:19
  5.2 3.6 %collective-permute-start.1 = (bf16[1,8,17,128]{3,2,1,0:T(8,128)(2,1)S(1)}, bf16[1,8,17,128]{3,2,1,0:T(8,128)(2,1)S(1)}, u32[]{:S(2)}, u32[]{:S(2)}) collective-permute-start(bf16[1,8,17,128]{3,2,1,0:T(8,128)(2,1)S(1)} %get-tuple-element.38), channel_id=1, source_target_pairs={{4,0},{8,4},{12,8},{16,12},{20,16},{24,20},{28,24},{32,28},{36,32}... | collective-permute-start | bytes 104456 | tf_op jit(solution)/shard_map/ppermute | solution.py:20
  8.9 0.8 broadcast_compare_fusion.30
  9.7 0.8 broadcast_compare_fusion.31
  10.5 0.8 slice_compare_fusion.3
  11.7 1.3 %collective-permute-start.2 = (bf16[4,1,17,128]{3,2,1,0:T(8,128)(2,1)S(1)}, bf16[4,1,17,128]{3,2,1,0:T(8,128)(2,1)S(1)}, u32[]{:S(2)}, u32[]{:S(2)}) collective-permute-start(bf16[4,1,17,128]{3,2,1,0:T(8,128)(2,1)S(1)} %get-tuple-element.23), channel_id=1, source_target_pairs={{1,0},{2,1},{3,2},{5,4},{6,5},{7,6},{9,8},{10,9},{11,10},{13,12},{... | collective-permute-start | bytes 52232 | tf_op jit(solution)/shard_map/ppermute | solution.py:20
  13.0 4.5 %collective-permute-start.3 = (bf16[4,1,17,128]{3,2,1,0:T(8,128)(2,1)S(1)}, bf16[4,1,17,128]{3,2,1,0:T(8,128)(2,1)S(1)}, u32[]{:S(2)}, u32[]{:S(2)}) collective-permute-start(bf16[4,1,17,128]{3,2,1,0:T(8,128)(2,1)S(1)} %get-tuple-element.24), channel_id=1, source_target_pairs={{0,1},{1,2},{2,3},{4,5},{5,6},{6,7},{8,9},{9,10},{10,11},{12,13},{... | collective-permute-start | bytes 52232 | tf_op jit(solution)/shard_map/ppermute | solution.py:19
  18.3 0.8 collective-permute-done.3
  19.1 0.2 select_select_fusion
  19.4 0.2 select_select_fusion.3
  19.7 0.2 select_select_fusion.2
  19.9 0.2 select_select_fusion.1
  20.2 0.7 fusion
  21.0 1.9 %collective-permute-start.4 = (bf16[1,8,16,128]{3,2,1,0:T(8,128)(2,1)S(1)}, bf16[1,8,16,128]{3,2,1,0:T(8,128)(2,1)S(1)}, u32[]{:S(2)}, u32[]{:S(2)}) collective-permute-start(bf16[1,8,16,128]{3,2,1,0:T(8,128)(2,1)S(1)} %get-tuple-element.43), channel_id=1, source_target_pairs={{0,4},{4,8},{8,12},{12,16},{16,20},{20,24},{24,28},{28,32},{32,36}... | collective-permute-start | bytes 98312 | tf_op jit(solution)/shard_map/ppermute | solution.py:19
  22.9 3.6 %collective-permute-start.5 = (bf16[1,8,16,128]{3,2,1,0:T(8,128)(2,1)S(1)}, bf16[1,8,16,128]{3,2,1,0:T(8,128)(2,1)S(1)}, u32[]{:S(2)}, u32[]{:S(2)}) collective-permute-start(bf16[1,8,16,128]{3,2,1,0:T(8,128)(2,1)S(1)} %get-tuple-element.44), channel_id=1, source_target_pairs={{4,0},{8,4},{12,8},{16,12},{20,16},{24,20},{28,24},{32,28},{36,32}... | collective-permute-start | bytes 98312 | tf_op jit(solution)/shard_map/ppermute | solution.py:20
  26.6 1.6 %collective-permute-done.5 = bf16[1,8,16,128]{3,2,1,0:T(8,128)(2,1)S(1)} collective-permute-done((bf16[1,8,16,128]{3,2,1,0:T(8,128)(2,1)S(1)}, bf16[1,8,16,128]{3,2,1,0:T(8,128)(2,1)S(1)}, u32[]{:S(2)}, u32[]{:S(2)}) %collective-permute-start.5) | collective-permute-done | bytes 32800 | tf_op jit(solution)/shard_map/ppermute | solution.py:20
  28.1 1.3 %collective-permute-start.6 = (bf16[4,1,16,128]{3,2,1,0:T(8,128)(2,1)S(1)}, bf16[4,1,16,128]{3,2,1,0:T(8,128)(2,1)S(1)}, u32[]{:S(2)}, u32[]{:S(2)}) collective-permute-start(bf16[4,1,16,128]{3,2,1,0:T(8,128)(2,1)S(1)} %get-tuple-element.35), channel_id=1, source_target_pairs={{1,0},{2,1},{3,2},{5,4},{6,5},{7,6},{9,8},{10,9},{11,10},{13,12},{... | collective-permute-start | bytes 49160 | tf_op jit(solution)/shard_map/ppermute | solution.py:20
  29.4 4.8 %collective-permute-start.7 = (bf16[4,1,16,128]{3,2,1,0:T(8,128)(2,1)S(1)}, bf16[4,1,16,128]{3,2,1,0:T(8,128)(2,1)S(1)}, u32[]{:S(2)}, u32[]{:S(2)}) collective-permute-start(bf16[4,1,16,128]{3,2,1,0:T(8,128)(2,1)S(1)} %get-tuple-element.36), channel_id=1, source_target_pairs={{0,1},{1,2},{2,3},{4,5},{5,6},{6,7},{8,9},{9,10},{10,11},{12,13},{... | collective-permute-start | bytes 49160 | tf_op jit(solution)/shard_map/ppermute | solution.py:19
  34.3 1.4 %collective-permute-done.7 = bf16[4,1,16,128]{3,2,1,0:T(8,128)(2,1)S(1)} collective-permute-done((bf16[4,1,16,128]{3,2,1,0:T(8,128)(2,1)S(1)}, bf16[4,1,16,128]{3,2,1,0:T(8,128)(2,1)S(1)}, u32[]{:S(2)}, u32[]{:S(2)}) %collective-permute-start.7) | collective-permute-done | bytes 16416 | tf_op jit(solution)/shard_map/ppermute | solution.py:19
  35.7 0.2 select_select_fusion.15
  36.0 0.2 select_select_fusion.13
  36.5 0.2 select_select_fusion.12
  36.7 0.6 fusion.8
  37.5 2.7 %collective-permute-start.8 = (bf16[1,8,16,128]{3,2,1,0:T(8,128)(2,1)S(1)}, bf16[1,8,16,128]{3,2,1,0:T(8,128)(2,1)S(1)}, u32[]{:S(2)}, u32[]{:S(2)}) collective-permute-start(bf16[1,8,16,128]{3,2,1,0:T(8,128)(2,1)S(1)} %get-tuple-element.41), channel_id=1, source_target_pairs={{0,4},{4,8},{8,12},{12,16},{16,20},{20,24},{24,28},{28,32},{32,36}... | collective-permute-start | bytes 98312 | tf_op jit(solution)/shard_map/ppermute | solution.py:19
  40.2 2.8 %collective-permute-start.9 = (bf16[1,8,16,128]{3,2,1,0:T(8,128)(2,1)S(1)}, bf16[1,8,16,128]{3,2,1,0:T(8,128)(2,1)S(1)}, u32[]{:S(2)}, u32[]{:S(2)}) collective-permute-start(bf16[1,8,16,128]{3,2,1,0:T(8,128)(2,1)S(1)} %get-tuple-element.42), channel_id=1, source_target_pairs={{4,0},{8,4},{12,8},{16,12},{20,16},{24,20},{28,24},{32,28},{36,32}... | collective-permute-start | bytes 98312 | tf_op jit(solution)/shard_map/ppermute | solution.py:20
  43.1 1.6 %collective-permute-done.9 = bf16[1,8,16,128]{3,2,1,0:T(8,128)(2,1)S(1)} collective-permute-done((bf16[1,8,16,128]{3,2,1,0:T(8,128)(2,1)S(1)}, bf16[1,8,16,128]{3,2,1,0:T(8,128)(2,1)S(1)}, u32[]{:S(2)}, u32[]{:S(2)}) %collective-permute-start.9) | collective-permute-done | bytes 32800 | tf_op jit(solution)/shard_map/ppermute | solution.py:20
  44.6 1.3 %collective-permute-start.10 = (bf16[4,1,16,128]{3,2,1,0:T(8,128)(2,1)S(1)}, bf16[4,1,16,128]{3,2,1,0:T(8,128)(2,1)S(1)}, u32[]{:S(2)}, u32[]{:S(2)}) collective-permute-start(bf16[4,1,16,128]{3,2,1,0:T(8,128)(2,1)S(1)} %get-tuple-element.31), channel_id=1, source_target_pairs={{1,0},{2,1},{3,2},{5,4},{6,5},{7,6},{9,8},{10,9},{11,10},{13,12},{... | collective-permute-start | bytes 49160 | tf_op jit(solution)/shard_map/ppermute | solution.py:20
  45.9 4.8 %collective-permute-start.11 = (bf16[4,1,16,128]{3,2,1,0:T(8,128)(2,1)S(1)}, bf16[4,1,16,128]{3,2,1,0:T(8,128)(2,1)S(1)}, u32[]{:S(2)}, u32[]{:S(2)}) collective-permute-start(bf16[4,1,16,128]{3,2,1,0:T(8,128)(2,1)S(1)} %get-tuple-element.32), channel_id=1, source_target_pairs={{0,1},{1,2},{2,3},{4,5},{5,6},{6,7},{8,9},{9,10},{10,11},{12,13},{... | collective-permute-start | bytes 49160 | tf_op jit(solution)/shard_map/ppermute | solution.py:19
  50.8 1.4 %collective-permute-done.11 = bf16[4,1,16,128]{3,2,1,0:T(8,128)(2,1)S(1)} collective-permute-done((bf16[4,1,16,128]{3,2,1,0:T(8,128)(2,1)S(1)}, bf16[4,1,16,128]{3,2,1,0:T(8,128)(2,1)S(1)}, u32[]{:S(2)}, u32[]{:S(2)}) %collective-permute-start.11) | collective-permute-done | bytes 16416 | tf_op jit(solution)/shard_map/ppermute | solution.py:19
  52.2 0.2 select_select_fusion.11
  53.2 0.6 fusion.16
  54.0 2.7 %collective-permute-start.12 = (bf16[1,8,16,128]{3,2,1,0:T(8,128)(2,1)S(1)}, bf16[1,8,16,128]{3,2,1,0:T(8,128)(2,1)S(1)}, u32[]{:S(2)}, u32[]{:S(2)}) collective-permute-start(bf16[1,8,16,128]{3,2,1,0:T(8,128)(2,1)S(1)} %get-tuple-element.39), channel_id=1, source_target_pairs={{0,4},{4,8},{8,12},{12,16},{16,20},{20,24},{24,28},{28,32},{32,36}... | collective-permute-start | bytes 98312 | tf_op jit(solution)/shard_map/ppermute | solution.py:19
  56.7 2.8 %collective-permute-start.13 = (bf16[1,8,16,128]{3,2,1,0:T(8,128)(2,1)S(1)}, bf16[1,8,16,128]{3,2,1,0:T(8,128)(2,1)S(1)}, u32[]{:S(2)}, u32[]{:S(2)}) collective-permute-start(bf16[1,8,16,128]{3,2,1,0:T(8,128)(2,1)S(1)} %get-tuple-element.40), channel_id=1, source_target_pairs={{4,0},{8,4},{12,8},{16,12},{20,16},{24,20},{28,24},{32,28},{36,32}... | collective-permute-start | bytes 98312 | tf_op jit(solution)/shard_map/ppermute | solution.py:20
  59.6 1.6 %collective-permute-done.13 = bf16[1,8,16,128]{3,2,1,0:T(8,128)(2,1)S(1)} collective-permute-done((bf16[1,8,16,128]{3,2,1,0:T(8,128)(2,1)S(1)}, bf16[1,8,16,128]{3,2,1,0:T(8,128)(2,1)S(1)}, u32[]{:S(2)}, u32[]{:S(2)}) %collective-permute-start.13) | collective-permute-done | bytes 32800 | tf_op jit(solution)/shard_map/ppermute | solution.py:20
  61.1 1.3 %collective-permute-start.14 = (bf16[4,1,16,128]{3,2,1,0:T(8,128)(2,1)S(1)}, bf16[4,1,16,128]{3,2,1,0:T(8,128)(2,1)S(1)}, u32[]{:S(2)}, u32[]{:S(2)}) collective-permute-start(bf16[4,1,16,128]{3,2,1,0:T(8,128)(2,1)S(1)} %get-tuple-element.27), channel_id=1, source_target_pairs={{1,0},{2,1},{3,2},{5,4},{6,5},{7,6},{9,8},{10,9},{11,10},{13,12},{... | collective-permute-start | bytes 49160 | tf_op jit(solution)/shard_map/ppermute | solution.py:20
  62.4 4.8 %collective-permute-start.15 = (bf16[4,1,16,128]{3,2,1,0:T(8,128)(2,1)S(1)}, bf16[4,1,16,128]{3,2,1,0:T(8,128)(2,1)S(1)}, u32[]{:S(2)}, u32[]{:S(2)}) collective-permute-start(bf16[4,1,16,128]{3,2,1,0:T(8,128)(2,1)S(1)} %get-tuple-element.28), channel_id=1, source_target_pairs={{0,1},{1,2},{2,3},{4,5},{5,6},{6,7},{8,9},{9,10},{10,11},{12,13},{... | collective-permute-start | bytes 49160 | tf_op jit(solution)/shard_map/ppermute | solution.py:19
  67.5 1.2 %collective-permute-done.15 = bf16[4,1,16,128]{3,2,1,0:T(8,128)(2,1)S(1)} collective-permute-done((bf16[4,1,16,128]{3,2,1,0:T(8,128)(2,1)S(1)}, bf16[4,1,16,128]{3,2,1,0:T(8,128)(2,1)S(1)}, u32[]{:S(2)}, u32[]{:S(2)}) %collective-permute-start.15) | collective-permute-done | bytes 16416 | tf_op jit(solution)/shard_map/ppermute | solution.py:19
  68.7 0.2 select_select_fusion.7
  69.7 0.6 fusion.24
  70.4 1.3 %multiply_reduce_fusion = (f32[6,16]{1,0:T(8,128)S(1)}, f32[6,2,8,16,128]{4,3,2,1,0:T(8,128)}) fusion(f32[2,8,16,128]{3,2,1,0:T(8,128)S(1)} %multiply_subtract_fusion, f32[6]{0:T(128)S(1)} %get-tuple-element.5, f32[2,8,16,128]{3,2,1,0:T(8,128)S(1)} %get-tuple-element.12, f32[6]{0:T(128)S(1)} %get-tuple-element.6, f32[2,8,16,128]{3,2,1,0:T(8,128)S(1)} %get-tuple-element.16, ...), kind=kLoop, calls=%fused_computation | loop fusion | flops 2162592 | bytes 1442296 | tf_op jit(solution)/shard_map/reduce_sum | solution.py:97
  71.7 10.5 %psum.28 = f32[6,16]{1,0:T(8,128)S(1)} all-reduce(f32[6,16]{1,0:T(8,128)S(1)} %get-tuple-element.7), channel_id=1, replica_groups=mesh['gx_0'=4,'gx_1'=4,'gx_2'=2,'gy'=4] {'gx_0'}, use_global_device_ids=true, to_apply=%region_1.2 | all-reduce | flops 96 | bytes 768 | tf_op jit(solution)/shard_map/psum | solution.py:27
  82.2 16.6 %psum.29 = f32[6,16]{1,0:T(8,128)S(1)} all-reduce(f32[6,16]{1,0:T(8,128)S(1)} %psum.28), channel_id=1, replica_groups=mesh['gx_0'=4,'gx_1'=4,'gx_2'=2,'gy'=4] {'gx_1'}, use_global_device_ids=true, to_apply=%region_2.3 | all-reduce | flops 96 | bytes 768 | tf_op jit(solution)/shard_map/psum | solution.py:27
  98.8 2.5 %psum.30 = f32[6,16]{1,0:T(8,128)S(1)} all-reduce(f32[6,16]{1,0:T(8,128)S(1)} %psum.29), channel_id=1, replica_groups=mesh['gx_0'=4,'gx_1'=4,'gx_2'=2,'gy'=4] {'gx_2'}, use_global_device_ids=true, to_apply=%region_3.4 | all-reduce | flops 96 | bytes 768 | tf_op jit(solution)/shard_map/psum | solution.py:27
  101.2 12.6 %psum.31 = f32[6,16]{1,0:T(8,128)S(1)} all-reduce(f32[6,16]{1,0:T(8,128)S(1)} %psum.30), channel_id=1, replica_groups=mesh['gx_0'=4,'gx_1'=4,'gx_2'=2,'gy'=4] {'gy'}, use_global_device_ids=true, to_apply=%region_4.5 | all-reduce | flops 96 | bytes 768 | tf_op jit(solution)/shard_map/psum | solution.py:27
  113.8 0.6 broadcast_multiply_fusion.2
  (63 shorter events, 2.6 us)
Async XLA Ops:
  0.6 19.6 %copy-start = (bf16[2,8,4,128,128]{4,3,2,1,0:T(8,128)(2,1)S(1)}, bf16[2,8,4,128,128]{4,3,2,1,0:T(8,128)(2,1)}, u32[]{:S(2)}) copy-start(bf16[2,8,4,128,128]{4,3,2,1,0:T(8,128)(2,1)} %param.9) | copy-start | bytes 6291460
  3.3 8.4 %collective-permute-start = (bf16[1,8,17,128]{3,2,1,0:T(8,128)(2,1)S(1)}, bf16[1,8,17,128]{3,2,1,0:T(8,128)(2,1)S(1)}, u32[]{:S(2)}, u32[]{:S(2)}) collective-permute-start(bf16[1,8,17,128]{3,2,1,0:T(8,128)(2,1)S(1)} %get-tuple-element.37), channel_id=1, source_target_pairs={{0,4},{4,8},{8,12},{12,16},{16,20},{20,24},{24,28},{28,32},{32,36}... | collective-permute-start | bytes 104456 | tf_op jit(solution)/shard_map/ppermute | solution.py:19
  5.2 6.4 %collective-permute-start.1 = (bf16[1,8,17,128]{3,2,1,0:T(8,128)(2,1)S(1)}, bf16[1,8,17,128]{3,2,1,0:T(8,128)(2,1)S(1)}, u32[]{:S(2)}, u32[]{:S(2)}) collective-permute-start(bf16[1,8,17,128]{3,2,1,0:T(8,128)(2,1)S(1)} %get-tuple-element.38), channel_id=1, source_target_pairs={{4,0},{8,4},{12,8},{16,12},{20,16},{24,20},{28,24},{32,28},{36,32}... | collective-permute-start | bytes 104456 | tf_op jit(solution)/shard_map/ppermute | solution.py:20
  11.7 6.6 %collective-permute-start.2 = (bf16[4,1,17,128]{3,2,1,0:T(8,128)(2,1)S(1)}, bf16[4,1,17,128]{3,2,1,0:T(8,128)(2,1)S(1)}, u32[]{:S(2)}, u32[]{:S(2)}) collective-permute-start(bf16[4,1,17,128]{3,2,1,0:T(8,128)(2,1)S(1)} %get-tuple-element.23), channel_id=1, source_target_pairs={{1,0},{2,1},{3,2},{5,4},{6,5},{7,6},{9,8},{10,9},{11,10},{13,12},{... | collective-permute-start | bytes 52232 | tf_op jit(solution)/shard_map/ppermute | solution.py:20
  13.0 6.1 %collective-permute-start.3 = (bf16[4,1,17,128]{3,2,1,0:T(8,128)(2,1)S(1)}, bf16[4,1,17,128]{3,2,1,0:T(8,128)(2,1)S(1)}, u32[]{:S(2)}, u32[]{:S(2)}) collective-permute-start(bf16[4,1,17,128]{3,2,1,0:T(8,128)(2,1)S(1)} %get-tuple-element.24), channel_id=1, source_target_pairs={{0,1},{1,2},{2,3},{4,5},{5,6},{6,7},{8,9},{9,10},{10,11},{12,13},{... | collective-permute-start | bytes 52232 | tf_op jit(solution)/shard_map/ppermute | solution.py:19
  19.9 1.0 copy-start.1
  21.0 5.6 %collective-permute-start.4 = (bf16[1,8,16,128]{3,2,1,0:T(8,128)(2,1)S(1)}, bf16[1,8,16,128]{3,2,1,0:T(8,128)(2,1)S(1)}, u32[]{:S(2)}, u32[]{:S(2)}) collective-permute-start(bf16[1,8,16,128]{3,2,1,0:T(8,128)(2,1)S(1)} %get-tuple-element.43), channel_id=1, source_target_pairs={{0,4},{4,8},{8,12},{12,16},{16,20},{20,24},{24,28},{28,32},{32,36}... | collective-permute-start | bytes 98312 | tf_op jit(solution)/shard_map/ppermute | solution.py:19
  22.9 5.2 %collective-permute-start.5 = (bf16[1,8,16,128]{3,2,1,0:T(8,128)(2,1)S(1)}, bf16[1,8,16,128]{3,2,1,0:T(8,128)(2,1)S(1)}, u32[]{:S(2)}, u32[]{:S(2)}) collective-permute-start(bf16[1,8,16,128]{3,2,1,0:T(8,128)(2,1)S(1)} %get-tuple-element.44), channel_id=1, source_target_pairs={{4,0},{8,4},{12,8},{16,12},{20,16},{24,20},{28,24},{32,28},{36,32}... | collective-permute-start | bytes 98312 | tf_op jit(solution)/shard_map/ppermute | solution.py:20
  28.1 6.1 %collective-permute-start.6 = (bf16[4,1,16,128]{3,2,1,0:T(8,128)(2,1)S(1)}, bf16[4,1,16,128]{3,2,1,0:T(8,128)(2,1)S(1)}, u32[]{:S(2)}, u32[]{:S(2)}) collective-permute-start(bf16[4,1,16,128]{3,2,1,0:T(8,128)(2,1)S(1)} %get-tuple-element.35), channel_id=1, source_target_pairs={{1,0},{2,1},{3,2},{5,4},{6,5},{7,6},{9,8},{10,9},{11,10},{13,12},{... | collective-permute-start | bytes 49160 | tf_op jit(solution)/shard_map/ppermute | solution.py:20
  29.4 6.3 %collective-permute-start.7 = (bf16[4,1,16,128]{3,2,1,0:T(8,128)(2,1)S(1)}, bf16[4,1,16,128]{3,2,1,0:T(8,128)(2,1)S(1)}, u32[]{:S(2)}, u32[]{:S(2)}) collective-permute-start(bf16[4,1,16,128]{3,2,1,0:T(8,128)(2,1)S(1)} %get-tuple-element.36), channel_id=1, source_target_pairs={{0,1},{1,2},{2,3},{4,5},{5,6},{6,7},{8,9},{9,10},{10,11},{12,13},{... | collective-permute-start | bytes 49160 | tf_op jit(solution)/shard_map/ppermute | solution.py:19
  37.5 5.6 %collective-permute-start.8 = (bf16[1,8,16,128]{3,2,1,0:T(8,128)(2,1)S(1)}, bf16[1,8,16,128]{3,2,1,0:T(8,128)(2,1)S(1)}, u32[]{:S(2)}, u32[]{:S(2)}) collective-permute-start(bf16[1,8,16,128]{3,2,1,0:T(8,128)(2,1)S(1)} %get-tuple-element.41), channel_id=1, source_target_pairs={{0,4},{4,8},{8,12},{12,16},{16,20},{20,24},{24,28},{28,32},{32,36}... | collective-permute-start | bytes 98312 | tf_op jit(solution)/shard_map/ppermute | solution.py:19
  40.2 4.4 %collective-permute-start.9 = (bf16[1,8,16,128]{3,2,1,0:T(8,128)(2,1)S(1)}, bf16[1,8,16,128]{3,2,1,0:T(8,128)(2,1)S(1)}, u32[]{:S(2)}, u32[]{:S(2)}) collective-permute-start(bf16[1,8,16,128]{3,2,1,0:T(8,128)(2,1)S(1)} %get-tuple-element.42), channel_id=1, source_target_pairs={{4,0},{8,4},{12,8},{16,12},{20,16},{24,20},{28,24},{32,28},{36,32}... | collective-permute-start | bytes 98312 | tf_op jit(solution)/shard_map/ppermute | solution.py:20
  44.6 6.1 %collective-permute-start.10 = (bf16[4,1,16,128]{3,2,1,0:T(8,128)(2,1)S(1)}, bf16[4,1,16,128]{3,2,1,0:T(8,128)(2,1)S(1)}, u32[]{:S(2)}, u32[]{:S(2)}) collective-permute-start(bf16[4,1,16,128]{3,2,1,0:T(8,128)(2,1)S(1)} %get-tuple-element.31), channel_id=1, source_target_pairs={{1,0},{2,1},{3,2},{5,4},{6,5},{7,6},{9,8},{10,9},{11,10},{13,12},{... | collective-permute-start | bytes 49160 | tf_op jit(solution)/shard_map/ppermute | solution.py:20
  45.9 6.3 %collective-permute-start.11 = (bf16[4,1,16,128]{3,2,1,0:T(8,128)(2,1)S(1)}, bf16[4,1,16,128]{3,2,1,0:T(8,128)(2,1)S(1)}, u32[]{:S(2)}, u32[]{:S(2)}) collective-permute-start(bf16[4,1,16,128]{3,2,1,0:T(8,128)(2,1)S(1)} %get-tuple-element.32), channel_id=1, source_target_pairs={{0,1},{1,2},{2,3},{4,5},{5,6},{6,7},{8,9},{9,10},{10,11},{12,13},{... | collective-permute-start | bytes 49160 | tf_op jit(solution)/shard_map/ppermute | solution.py:19
  53.0 14.3 %copy-start.2 = (f32[6,5]{1,0:T(8,128)S(1)}, f32[6,5]{1,0:T(8,128)}, u32[]{:S(2)}) copy-start(f32[6,5]{1,0:T(8,128)} %param.14) | copy-start | bytes 364
  54.0 5.6 %collective-permute-start.12 = (bf16[1,8,16,128]{3,2,1,0:T(8,128)(2,1)S(1)}, bf16[1,8,16,128]{3,2,1,0:T(8,128)(2,1)S(1)}, u32[]{:S(2)}, u32[]{:S(2)}) collective-permute-start(bf16[1,8,16,128]{3,2,1,0:T(8,128)(2,1)S(1)} %get-tuple-element.39), channel_id=1, source_target_pairs={{0,4},{4,8},{8,12},{12,16},{16,20},{20,24},{24,28},{28,32},{32,36}... | collective-permute-start | bytes 98312 | tf_op jit(solution)/shard_map/ppermute | solution.py:19
  56.7 4.4 %collective-permute-start.13 = (bf16[1,8,16,128]{3,2,1,0:T(8,128)(2,1)S(1)}, bf16[1,8,16,128]{3,2,1,0:T(8,128)(2,1)S(1)}, u32[]{:S(2)}, u32[]{:S(2)}) collective-permute-start(bf16[1,8,16,128]{3,2,1,0:T(8,128)(2,1)S(1)} %get-tuple-element.40), channel_id=1, source_target_pairs={{4,0},{8,4},{12,8},{16,12},{20,16},{24,20},{28,24},{32,28},{36,32}... | collective-permute-start | bytes 98312 | tf_op jit(solution)/shard_map/ppermute | solution.py:20
  61.1 6.4 %collective-permute-start.14 = (bf16[4,1,16,128]{3,2,1,0:T(8,128)(2,1)S(1)}, bf16[4,1,16,128]{3,2,1,0:T(8,128)(2,1)S(1)}, u32[]{:S(2)}, u32[]{:S(2)}) collective-permute-start(bf16[4,1,16,128]{3,2,1,0:T(8,128)(2,1)S(1)} %get-tuple-element.27), channel_id=1, source_target_pairs={{1,0},{2,1},{3,2},{5,4},{6,5},{7,6},{9,8},{10,9},{11,10},{13,12},{... | collective-permute-start | bytes 49160 | tf_op jit(solution)/shard_map/ppermute | solution.py:20
  62.4 6.3 %collective-permute-start.15 = (bf16[4,1,16,128]{3,2,1,0:T(8,128)(2,1)S(1)}, bf16[4,1,16,128]{3,2,1,0:T(8,128)(2,1)S(1)}, u32[]{:S(2)}, u32[]{:S(2)}) collective-permute-start(bf16[4,1,16,128]{3,2,1,0:T(8,128)(2,1)S(1)} %get-tuple-element.28), channel_id=1, source_target_pairs={{0,1},{1,2},{2,3},{4,5},{5,6},{6,7},{8,9},{9,10},{10,11},{12,13},{... | collective-permute-start | bytes 49160 | tf_op jit(solution)/shard_map/ppermute | solution.py:19
where the time goes:
time: 115 us; the launch traced here: 114 us
  starting transfers between devices  46.4 us (40%)
  blocking collectives  42.1 us (37%)
  other arithmetic  11.6 us (10%)
  waiting for transfers between devices  9.5 us (8%)
  matrix products  2.6 us (2%)
  between operations  1.98 us (2%)
    psum x4, blocking collectives, over_axes(): array = lax.psum(array, axis)  42.1 us
    ppermute x8, starting transfers between devices, with_halo(): before = lax.ppermute(last, axis, up)  28.4 us
    ppermute x8, starting transfers between devices, with_halo(): after = lax.ppermute(first, axis, down)  18.1 us
    ppermute x8, waiting for transfers between devices, with_halo(): before = lax.ppermute(last, axis, up)  4.79 us
    ppermute x8, waiting for transfers between devices, with_halo(): after = lax.ppermute(first, axis, down)  4.71 us
    select_n x16, other arithmetic, adjacency(): picked = jnp.where(kept, picked, jnp.zeros_like(picked))  3.91 us
    dot_general x4, matrix products, adjacency(): lax.dot_general(flat_inputs, flat_tiles, (((1, 3), (1, 3)), ((0,), (0,)))...  2.6 us
  transfers between devices with their start and end apart: 16, of which 7 were waited for; matrix products, arithmetic and copies ran while one was open for 3% of the time, Pallas kernels for 0%

commit v1 on v0

--- a/solution.py
+++ b/solution.py
@@ -24,7 +24,7 @@
 
 def over_axes(array, axes):
     for axis in axes:
-        array = lax.psum(array, axis)
+        array = jnp.sum(lax.all_gather(array, axis), axis=0)
     return array
 
 

time: 115 us -> 121 us (1.052)
  the two profiles are of different devices: /device:TPU:8 before, /device:TPU:0 now
where the time goes in v1:
time: 121 us
  blocking collectives  49.3 us (41%)
  starting transfers between devices  41.7 us (34%)
  waiting for transfers between devices  13.4 us (11%)
  other arithmetic  11.6 us (10%)
  matrix products  2.6 us (2%)
  between operations  1.97 us (2%)
    all_gather x4, blocking collectives, over_axes(): array = jnp.sum(lax.all_gather(array, axis), axis=0)  49.3 us
    ppermute x8, starting transfers between devices, with_halo(): before = lax.ppermute(last, axis, up)  31.4 us
    ppermute x8, starting transfers between devices, with_halo(): after = lax.ppermute(first, axis, down)  10.3 us
    ppermute x8, waiting for transfers between devices, with_halo(): after = lax.ppermute(first, axis, down)  8.58 us
    ppermute x8, waiting for transfers between devices, with_halo(): before = lax.ppermute(last, axis, up)  4.79 us
    select_n x16, other arithmetic, adjacency(): picked = jnp.where(kept, picked, jnp.zeros_like(picked))  3.91 us
    dot_general x4, matrix products, adjacency(): lax.dot_general(flat_inputs, flat_tiles, (((1, 3), (1, 3)), ((0,), (0,)))...  2.6 us
  transfers between devices with their start and end apart: 16, of which 8 were waited for; matrix products, arithmetic and copies ran while one was open for 2% of the time, Pallas kernels for 0%

profile of v1, /device:TPU:0, one launch (start us, length us, event | category | flops | bytes accessed | tf_op | source)
XLA Modules:
  0.0 120.8 jit_solution(11165109094340873988)
XLA Ops:
  0.6 0.9 compare_convert_fusion
  1.6 0.8 fusion.35
  2.3 0.9 broadcast_multiply_fusion.1
  3.3 1.3 %collective-permute-start = (bf16[1,8,17,128]{3,2,1,0:T(8,128)(2,1)S(1)}, bf16[1,8,17,128]{3,2,1,0:T(8,128)(2,1)S(1)}, u32[]{:S(2)}, u32[]{:S(2)}) collective-permute-start(bf16[1,8,17,128]{3,2,1,0:T(8,128)(2,1)S(1)} %get-tuple-element.37), channel_id=1, source_target_pairs={{0,4},{4,8},{8,12},{12,16},{16,20},{20,24},{24,28},{28,32},{32,36}... | collective-permute-start | bytes 104456 | tf_op jit(solution)/shard_map/ppermute | solution.py:19
  4.6 1.3 %collective-permute-start.1 = (bf16[1,8,17,128]{3,2,1,0:T(8,128)(2,1)S(1)}, bf16[1,8,17,128]{3,2,1,0:T(8,128)(2,1)S(1)}, u32[]{:S(2)}, u32[]{:S(2)}) collective-permute-start(bf16[1,8,17,128]{3,2,1,0:T(8,128)(2,1)S(1)} %get-tuple-element.38), channel_id=1, source_target_pairs={{4,0},{8,4},{12,8},{16,12},{20,16},{24,20},{28,24},{32,28},{36,32}... | collective-permute-start | bytes 104456 | tf_op jit(solution)/shard_map/ppermute | solution.py:20
  5.9 0.8 broadcast_compare_fusion.30
  6.7 0.8 broadcast_compare_fusion.31
  7.6 0.8 slice_compare_fusion.3
  8.7 1.0 collective-permute-done.1
  9.7 1.3 %collective-permute-start.2 = (bf16[4,1,17,128]{3,2,1,0:T(8,128)(2,1)S(1)}, bf16[4,1,17,128]{3,2,1,0:T(8,128)(2,1)S(1)}, u32[]{:S(2)}, u32[]{:S(2)}) collective-permute-start(bf16[4,1,17,128]{3,2,1,0:T(8,128)(2,1)S(1)} %get-tuple-element.23), channel_id=1, source_target_pairs={{1,0},{2,1},{3,2},{5,4},{6,5},{7,6},{9,8},{10,9},{11,10},{13,12},{... | collective-permute-start | bytes 52232 | tf_op jit(solution)/shard_map/ppermute | solution.py:20
  11.0 4.5 %collective-permute-start.3 = (bf16[4,1,17,128]{3,2,1,0:T(8,128)(2,1)S(1)}, bf16[4,1,17,128]{3,2,1,0:T(8,128)(2,1)S(1)}, u32[]{:S(2)}, u32[]{:S(2)}) collective-permute-start(bf16[4,1,17,128]{3,2,1,0:T(8,128)(2,1)S(1)} %get-tuple-element.24), channel_id=1, source_target_pairs={{0,1},{1,2},{2,3},{4,5},{5,6},{6,7},{8,9},{9,10},{10,11},{12,13},{... | collective-permute-start | bytes 52232 | tf_op jit(solution)/shard_map/ppermute | solution.py:19
  16.3 0.8 collective-permute-done.3
  17.1 0.2 select_select_fusion
  17.4 0.2 select_select_fusion.3
  17.6 0.2 select_select_fusion.2
  17.9 0.2 select_select_fusion.1
  18.2 0.7 fusion
  18.9 3.7 %collective-permute-start.4 = (bf16[1,8,16,128]{3,2,1,0:T(8,128)(2,1)S(1)}, bf16[1,8,16,128]{3,2,1,0:T(8,128)(2,1)S(1)}, u32[]{:S(2)}, u32[]{:S(2)}) collective-permute-start(bf16[1,8,16,128]{3,2,1,0:T(8,128)(2,1)S(1)} %get-tuple-element.43), channel_id=1, source_target_pairs={{0,4},{4,8},{8,12},{12,16},{16,20},{20,24},{24,28},{28,32},{32,36}... | collective-permute-start | bytes 98312 | tf_op jit(solution)/shard_map/ppermute | solution.py:19
  22.7 1.3 %collective-permute-start.5 = (bf16[1,8,16,128]{3,2,1,0:T(8,128)(2,1)S(1)}, bf16[1,8,16,128]{3,2,1,0:T(8,128)(2,1)S(1)}, u32[]{:S(2)}, u32[]{:S(2)}) collective-permute-start(bf16[1,8,16,128]{3,2,1,0:T(8,128)(2,1)S(1)} %get-tuple-element.44), channel_id=1, source_target_pairs={{4,0},{8,4},{12,8},{16,12},{20,16},{24,20},{28,24},{32,28},{36,32}... | collective-permute-start | bytes 98312 | tf_op jit(solution)/shard_map/ppermute | solution.py:20
  24.0 3.3 %collective-permute-done.5 = bf16[1,8,16,128]{3,2,1,0:T(8,128)(2,1)S(1)} collective-permute-done((bf16[1,8,16,128]{3,2,1,0:T(8,128)(2,1)S(1)}, bf16[1,8,16,128]{3,2,1,0:T(8,128)(2,1)S(1)}, u32[]{:S(2)}, u32[]{:S(2)}) %collective-permute-start.5) | collective-permute-done | bytes 32800 | tf_op jit(solution)/shard_map/ppermute | solution.py:20
  27.3 1.3 %collective-permute-start.6 = (bf16[4,1,16,128]{3,2,1,0:T(8,128)(2,1)S(1)}, bf16[4,1,16,128]{3,2,1,0:T(8,128)(2,1)S(1)}, u32[]{:S(2)}, u32[]{:S(2)}) collective-permute-start(bf16[4,1,16,128]{3,2,1,0:T(8,128)(2,1)S(1)} %get-tuple-element.35), channel_id=1, source_target_pairs={{1,0},{2,1},{3,2},{5,4},{6,5},{7,6},{9,8},{10,9},{11,10},{13,12},{... | collective-permute-start | bytes 49160 | tf_op jit(solution)/shard_map/ppermute | solution.py:20
  28.6 4.8 %collective-permute-start.7 = (bf16[4,1,16,128]{3,2,1,0:T(8,128)(2,1)S(1)}, bf16[4,1,16,128]{3,2,1,0:T(8,128)(2,1)S(1)}, u32[]{:S(2)}, u32[]{:S(2)}) collective-permute-start(bf16[4,1,16,128]{3,2,1,0:T(8,128)(2,1)S(1)} %get-tuple-element.36), channel_id=1, source_target_pairs={{0,1},{1,2},{2,3},{4,5},{5,6},{6,7},{8,9},{9,10},{10,11},{12,13},{... | collective-permute-start | bytes 49160 | tf_op jit(solution)/shard_map/ppermute | solution.py:19
  33.5 1.4 %collective-permute-done.7 = bf16[4,1,16,128]{3,2,1,0:T(8,128)(2,1)S(1)} collective-permute-done((bf16[4,1,16,128]{3,2,1,0:T(8,128)(2,1)S(1)}, bf16[4,1,16,128]{3,2,1,0:T(8,128)(2,1)S(1)}, u32[]{:S(2)}, u32[]{:S(2)}) %collective-permute-start.7) | collective-permute-done | bytes 16416 | tf_op jit(solution)/shard_map/ppermute | solution.py:19
  34.9 0.2 select_select_fusion.15
  35.2 0.2 select_select_fusion.13
  35.9 0.6 fusion.8
  36.7 3.7 %collective-permute-start.8 = (bf16[1,8,16,128]{3,2,1,0:T(8,128)(2,1)S(1)}, bf16[1,8,16,128]{3,2,1,0:T(8,128)(2,1)S(1)}, u32[]{:S(2)}, u32[]{:S(2)}) collective-permute-start(bf16[1,8,16,128]{3,2,1,0:T(8,128)(2,1)S(1)} %get-tuple-element.41), channel_id=1, source_target_pairs={{0,4},{4,8},{8,12},{12,16},{16,20},{20,24},{24,28},{28,32},{32,36}... | collective-permute-start | bytes 98312 | tf_op jit(solution)/shard_map/ppermute | solution.py:19
  40.3 1.3 %collective-permute-start.9 = (bf16[1,8,16,128]{3,2,1,0:T(8,128)(2,1)S(1)}, bf16[1,8,16,128]{3,2,1,0:T(8,128)(2,1)S(1)}, u32[]{:S(2)}, u32[]{:S(2)}) collective-permute-start(bf16[1,8,16,128]{3,2,1,0:T(8,128)(2,1)S(1)} %get-tuple-element.42), channel_id=1, source_target_pairs={{4,0},{8,4},{12,8},{16,12},{20,16},{24,20},{28,24},{32,28},{36,32}... | collective-permute-start | bytes 98312 | tf_op jit(solution)/shard_map/ppermute | solution.py:20
  41.7 2.2 %collective-permute-done.9 = bf16[1,8,16,128]{3,2,1,0:T(8,128)(2,1)S(1)} collective-permute-done((bf16[1,8,16,128]{3,2,1,0:T(8,128)(2,1)S(1)}, bf16[1,8,16,128]{3,2,1,0:T(8,128)(2,1)S(1)}, u32[]{:S(2)}, u32[]{:S(2)}) %collective-permute-start.9) | collective-permute-done | bytes 32800 | tf_op jit(solution)/shard_map/ppermute | solution.py:20
  43.8 1.3 %collective-permute-start.10 = (bf16[4,1,16,128]{3,2,1,0:T(8,128)(2,1)S(1)}, bf16[4,1,16,128]{3,2,1,0:T(8,128)(2,1)S(1)}, u32[]{:S(2)}, u32[]{:S(2)}) collective-permute-start(bf16[4,1,16,128]{3,2,1,0:T(8,128)(2,1)S(1)} %get-tuple-element.31), channel_id=1, source_target_pairs={{1,0},{2,1},{3,2},{5,4},{6,5},{7,6},{9,8},{10,9},{11,10},{13,12},{... | collective-permute-start | bytes 49160 | tf_op jit(solution)/shard_map/ppermute | solution.py:20
  45.1 4.8 %collective-permute-start.11 = (bf16[4,1,16,128]{3,2,1,0:T(8,128)(2,1)S(1)}, bf16[4,1,16,128]{3,2,1,0:T(8,128)(2,1)S(1)}, u32[]{:S(2)}, u32[]{:S(2)}) collective-permute-start(bf16[4,1,16,128]{3,2,1,0:T(8,128)(2,1)S(1)} %get-tuple-element.32), channel_id=1, source_target_pairs={{0,1},{1,2},{2,3},{4,5},{5,6},{6,7},{8,9},{9,10},{10,11},{12,13},{... | collective-permute-start | bytes 49160 | tf_op jit(solution)/shard_map/ppermute | solution.py:19
  49.9 1.4 %collective-permute-done.11 = bf16[4,1,16,128]{3,2,1,0:T(8,128)(2,1)S(1)} collective-permute-done((bf16[4,1,16,128]{3,2,1,0:T(8,128)(2,1)S(1)}, bf16[4,1,16,128]{3,2,1,0:T(8,128)(2,1)S(1)}, u32[]{:S(2)}, u32[]{:S(2)}) %collective-permute-start.11) | collective-permute-done | bytes 16416 | tf_op jit(solution)/shard_map/ppermute | solution.py:19
  51.4 0.2 select_select_fusion.11
  52.4 0.6 fusion.16
  53.1 3.7 %collective-permute-start.12 = (bf16[1,8,16,128]{3,2,1,0:T(8,128)(2,1)S(1)}, bf16[1,8,16,128]{3,2,1,0:T(8,128)(2,1)S(1)}, u32[]{:S(2)}, u32[]{:S(2)}) collective-permute-start(bf16[1,8,16,128]{3,2,1,0:T(8,128)(2,1)S(1)} %get-tuple-element.39), channel_id=1, source_target_pairs={{0,4},{4,8},{8,12},{12,16},{16,20},{20,24},{24,28},{28,32},{32,36}... | collective-permute-start | bytes 98312 | tf_op jit(solution)/shard_map/ppermute | solution.py:19
  56.8 1.3 %collective-permute-start.13 = (bf16[1,8,16,128]{3,2,1,0:T(8,128)(2,1)S(1)}, bf16[1,8,16,128]{3,2,1,0:T(8,128)(2,1)S(1)}, u32[]{:S(2)}, u32[]{:S(2)}) collective-permute-start(bf16[1,8,16,128]{3,2,1,0:T(8,128)(2,1)S(1)} %get-tuple-element.40), channel_id=1, source_target_pairs={{4,0},{8,4},{12,8},{16,12},{20,16},{24,20},{28,24},{32,28},{36,32}... | collective-permute-start | bytes 98312 | tf_op jit(solution)/shard_map/ppermute | solution.py:20
  58.1 2.2 %collective-permute-done.13 = bf16[1,8,16,128]{3,2,1,0:T(8,128)(2,1)S(1)} collective-permute-done((bf16[1,8,16,128]{3,2,1,0:T(8,128)(2,1)S(1)}, bf16[1,8,16,128]{3,2,1,0:T(8,128)(2,1)S(1)}, u32[]{:S(2)}, u32[]{:S(2)}) %collective-permute-start.13) | collective-permute-done | bytes 32800 | tf_op jit(solution)/shard_map/ppermute | solution.py:20
  60.3 1.3 %collective-permute-start.14 = (bf16[4,1,16,128]{3,2,1,0:T(8,128)(2,1)S(1)}, bf16[4,1,16,128]{3,2,1,0:T(8,128)(2,1)S(1)}, u32[]{:S(2)}, u32[]{:S(2)}) collective-permute-start(bf16[4,1,16,128]{3,2,1,0:T(8,128)(2,1)S(1)} %get-tuple-element.27), channel_id=1, source_target_pairs={{1,0},{2,1},{3,2},{5,4},{6,5},{7,6},{9,8},{10,9},{11,10},{13,12},{... | collective-permute-start | bytes 49160 | tf_op jit(solution)/shard_map/ppermute | solution.py:20
  61.6 4.8 %collective-permute-start.15 = (bf16[4,1,16,128]{3,2,1,0:T(8,128)(2,1)S(1)}, bf16[4,1,16,128]{3,2,1,0:T(8,128)(2,1)S(1)}, u32[]{:S(2)}, u32[]{:S(2)}) collective-permute-start(bf16[4,1,16,128]{3,2,1,0:T(8,128)(2,1)S(1)} %get-tuple-element.28), channel_id=1, source_target_pairs={{0,1},{1,2},{2,3},{4,5},{5,6},{6,7},{8,9},{9,10},{10,11},{12,13},{... | collective-permute-start | bytes 49160 | tf_op jit(solution)/shard_map/ppermute | solution.py:19
  66.7 1.2 collective-permute-done.15
  67.9 0.2 select_select_fusion.7
  68.9 0.6 fusion.24
  69.6 1.3 %multiply_reduce_fusion = (f32[6,16]{1,0:T(8,128)S(1)}, f32[6,2,8,16,128]{4,3,2,1,0:T(8,128)}) fusion(f32[2,8,16,128]{3,2,1,0:T(8,128)S(1)} %multiply_subtract_fusion, f32[6]{0:T(128)S(1)} %get-tuple-element.5, f32[2,8,16,128]{3,2,1,0:T(8,128)S(1)} %get-tuple-element.12, f32[6]{0:T(128)S(1)} %get-tuple-element.6, f32[2,8,16,128]{3,2,1,0:T(8,128)S(1)} %get-tuple-element.16, ...), kind=kLoop, calls=%fused_computation | loop fusion | flops 2162592 | bytes 1442296 | tf_op jit(solution)/shard_map/reduce_sum | solution.py:97
  70.9 21.7 %all-gather.4 = f32[4,6,16]{2,1,0:T(8,128)S(1)} all-gather(f32[1,6,16]{2,1,0:T(8,128)S(1)} %bitcast.153), channel_id=2, replica_groups=mesh['gx_0'=4,'gx_1'=4,'gx_2'=2,'gy'=4] {'gx_0'}, dimensions={0}, use_global_device_ids=true | all-gather | bytes 1920 | tf_op jit(solution)/shard_map/all_gather | solution.py:27
  92.6 12.0 %all-gather.5 = f32[4,6,16]{2,1,0:T(8,128)S(1)} all-gather(f32[1,6,16]{2,1,0:T(8,128)S(1)} %bitcast.155), channel_id=3, replica_groups=mesh['gx_0'=4,'gx_1'=4,'gx_2'=2,'gy'=4] {'gx_1'}, dimensions={0}, use_global_device_ids=true | all-gather | bytes 1920 | tf_op jit(solution)/shard_map/all_gather | solution.py:27
  104.6 1.8 %all-gather.6 = f32[2,6,16]{2,1,0:T(8,128)S(1)} all-gather(f32[1,6,16]{2,1,0:T(8,128)S(1)} %bitcast.156), channel_id=4, replica_groups=mesh['gx_0'=4,'gx_1'=4,'gx_2'=2,'gy'=4] {'gx_2'}, dimensions={0}, use_global_device_ids=true | all-gather | bytes 1152 | tf_op jit(solution)/shard_map/all_gather | solution.py:27
  106.5 13.7 %all-gather.7 = f32[4,6,16]{2,1,0:T(8,128)S(1)} all-gather(f32[1,6,16]{2,1,0:T(8,128)S(1)} %bitcast.154), channel_id=5, replica_groups=mesh['gx_0'=4,'gx_1'=4,'gx_2'=2,'gy'=4] {'gy'}, dimensions={0}, use_global_device_ids=true | all-gather | bytes 1920 | tf_op jit(solution)/shard_map/all_gather | solution.py:27
  120.2 0.6 broadcast_multiply_fusion.2
  (67 shorter events, 2.9 us)
Async XLA Ops:
  0.6 17.5 %copy-start = (bf16[2,8,4,128,128]{4,3,2,1,0:T(8,128)(2,1)S(1)}, bf16[2,8,4,128,128]{4,3,2,1,0:T(8,128)(2,1)}, u32[]{:S(2)}) copy-start(bf16[2,8,4,128,128]{4,3,2,1,0:T(8,128)(2,1)} %param.9) | copy-start | bytes 6291460
  3.3 5.4 %collective-permute-start = (bf16[1,8,17,128]{3,2,1,0:T(8,128)(2,1)S(1)}, bf16[1,8,17,128]{3,2,1,0:T(8,128)(2,1)S(1)}, u32[]{:S(2)}, u32[]{:S(2)}) collective-permute-start(bf16[1,8,17,128]{3,2,1,0:T(8,128)(2,1)S(1)} %get-tuple-element.37), channel_id=1, source_target_pairs={{0,4},{4,8},{8,12},{12,16},{16,20},{20,24},{24,28},{28,32},{32,36}... | collective-permute-start | bytes 104456 | tf_op jit(solution)/shard_map/ppermute | solution.py:19
  4.6 5.0 %collective-permute-start.1 = (bf16[1,8,17,128]{3,2,1,0:T(8,128)(2,1)S(1)}, bf16[1,8,17,128]{3,2,1,0:T(8,128)(2,1)S(1)}, u32[]{:S(2)}, u32[]{:S(2)}) collective-permute-start(bf16[1,8,17,128]{3,2,1,0:T(8,128)(2,1)S(1)} %get-tuple-element.38), channel_id=1, source_target_pairs={{4,0},{8,4},{12,8},{16,12},{20,16},{24,20},{28,24},{32,28},{36,32}... | collective-permute-start | bytes 104456 | tf_op jit(solution)/shard_map/ppermute | solution.py:20
  9.7 6.6 %collective-permute-start.2 = (bf16[4,1,17,128]{3,2,1,0:T(8,128)(2,1)S(1)}, bf16[4,1,17,128]{3,2,1,0:T(8,128)(2,1)S(1)}, u32[]{:S(2)}, u32[]{:S(2)}) collective-permute-start(bf16[4,1,17,128]{3,2,1,0:T(8,128)(2,1)S(1)} %get-tuple-element.23), channel_id=1, source_target_pairs={{1,0},{2,1},{3,2},{5,4},{6,5},{7,6},{9,8},{10,9},{11,10},{13,12},{... | collective-permute-start | bytes 52232 | tf_op jit(solution)/shard_map/ppermute | solution.py:20
  11.0 6.1 %collective-permute-start.3 = (bf16[4,1,17,128]{3,2,1,0:T(8,128)(2,1)S(1)}, bf16[4,1,17,128]{3,2,1,0:T(8,128)(2,1)S(1)}, u32[]{:S(2)}, u32[]{:S(2)}) collective-permute-start(bf16[4,1,17,128]{3,2,1,0:T(8,128)(2,1)S(1)} %get-tuple-element.24), channel_id=1, source_target_pairs={{0,1},{1,2},{2,3},{4,5},{5,6},{6,7},{8,9},{9,10},{10,11},{12,13},{... | collective-permute-start | bytes 52232 | tf_op jit(solution)/shard_map/ppermute | solution.py:19
  17.9 1.0 copy-start.1
  18.9 5.0 %collective-permute-start.4 = (bf16[1,8,16,128]{3,2,1,0:T(8,128)(2,1)S(1)}, bf16[1,8,16,128]{3,2,1,0:T(8,128)(2,1)S(1)}, u32[]{:S(2)}, u32[]{:S(2)}) collective-permute-start(bf16[1,8,16,128]{3,2,1,0:T(8,128)(2,1)S(1)} %get-tuple-element.43), channel_id=1, source_target_pairs={{0,4},{4,8},{8,12},{12,16},{16,20},{20,24},{24,28},{28,32},{32,36}... | collective-permute-start | bytes 98312 | tf_op jit(solution)/shard_map/ppermute | solution.py:19
  22.7 4.6 %collective-permute-start.5 = (bf16[1,8,16,128]{3,2,1,0:T(8,128)(2,1)S(1)}, bf16[1,8,16,128]{3,2,1,0:T(8,128)(2,1)S(1)}, u32[]{:S(2)}, u32[]{:S(2)}) collective-permute-start(bf16[1,8,16,128]{3,2,1,0:T(8,128)(2,1)S(1)} %get-tuple-element.44), channel_id=1, source_target_pairs={{4,0},{8,4},{12,8},{16,12},{20,16},{24,20},{28,24},{32,28},{36,32}... | collective-permute-start | bytes 98312 | tf_op jit(solution)/shard_map/ppermute | solution.py:20
  27.3 6.1 %collective-permute-start.6 = (bf16[4,1,16,128]{3,2,1,0:T(8,128)(2,1)S(1)}, bf16[4,1,16,128]{3,2,1,0:T(8,128)(2,1)S(1)}, u32[]{:S(2)}, u32[]{:S(2)}) collective-permute-start(bf16[4,1,16,128]{3,2,1,0:T(8,128)(2,1)S(1)} %get-tuple-element.35), channel_id=1, source_target_pairs={{1,0},{2,1},{3,2},{5,4},{6,5},{7,6},{9,8},{10,9},{11,10},{13,12},{... | collective-permute-start | bytes 49160 | tf_op jit(solution)/shard_map/ppermute | solution.py:20
  28.6 6.3 %collective-permute-start.7 = (bf16[4,1,16,128]{3,2,1,0:T(8,128)(2,1)S(1)}, bf16[4,1,16,128]{3,2,1,0:T(8,128)(2,1)S(1)}, u32[]{:S(2)}, u32[]{:S(2)}) collective-permute-start(bf16[4,1,16,128]{3,2,1,0:T(8,128)(2,1)S(1)} %get-tuple-element.36), channel_id=1, source_target_pairs={{0,1},{1,2},{2,3},{4,5},{5,6},{6,7},{8,9},{9,10},{10,11},{12,13},{... | collective-permute-start | bytes 49160 | tf_op jit(solution)/shard_map/ppermute | solution.py:19
  36.7 5.0 %collective-permute-start.8 = (bf16[1,8,16,128]{3,2,1,0:T(8,128)(2,1)S(1)}, bf16[1,8,16,128]{3,2,1,0:T(8,128)(2,1)S(1)}, u32[]{:S(2)}, u32[]{:S(2)}) collective-permute-start(bf16[1,8,16,128]{3,2,1,0:T(8,128)(2,1)S(1)} %get-tuple-element.41), channel_id=1, source_target_pairs={{0,4},{4,8},{8,12},{12,16},{16,20},{20,24},{24,28},{28,32},{32,36}... | collective-permute-start | bytes 98312 | tf_op jit(solution)/shard_map/ppermute | solution.py:19
  40.3 3.5 %collective-permute-start.9 = (bf16[1,8,16,128]{3,2,1,0:T(8,128)(2,1)S(1)}, bf16[1,8,16,128]{3,2,1,0:T(8,128)(2,1)S(1)}, u32[]{:S(2)}, u32[]{:S(2)}) collective-permute-start(bf16[1,8,16,128]{3,2,1,0:T(8,128)(2,1)S(1)} %get-tuple-element.42), channel_id=1, source_target_pairs={{4,0},{8,4},{12,8},{16,12},{20,16},{24,20},{28,24},{32,28},{36,32}... | collective-permute-start | bytes 98312 | tf_op jit(solution)/shard_map/ppermute | solution.py:20
  43.8 6.1 %collective-permute-start.10 = (bf16[4,1,16,128]{3,2,1,0:T(8,128)(2,1)S(1)}, bf16[4,1,16,128]{3,2,1,0:T(8,128)(2,1)S(1)}, u32[]{:S(2)}, u32[]{:S(2)}) collective-permute-start(bf16[4,1,16,128]{3,2,1,0:T(8,128)(2,1)S(1)} %get-tuple-element.31), channel_id=1, source_target_pairs={{1,0},{2,1},{3,2},{5,4},{6,5},{7,6},{9,8},{10,9},{11,10},{13,12},{... | collective-permute-start | bytes 49160 | tf_op jit(solution)/shard_map/ppermute | solution.py:20
  45.1 6.3 %collective-permute-start.11 = (bf16[4,1,16,128]{3,2,1,0:T(8,128)(2,1)S(1)}, bf16[4,1,16,128]{3,2,1,0:T(8,128)(2,1)S(1)}, u32[]{:S(2)}, u32[]{:S(2)}) collective-permute-start(bf16[4,1,16,128]{3,2,1,0:T(8,128)(2,1)S(1)} %get-tuple-element.32), channel_id=1, source_target_pairs={{0,1},{1,2},{2,3},{4,5},{5,6},{6,7},{8,9},{9,10},{10,11},{12,13},{... | collective-permute-start | bytes 49160 | tf_op jit(solution)/shard_map/ppermute | solution.py:19
  52.1 14.3 %copy-start.2 = (f32[6,5]{1,0:T(8,128)S(1)}, f32[6,5]{1,0:T(8,128)}, u32[]{:S(2)}) copy-start(f32[6,5]{1,0:T(8,128)} %param.14) | copy-start | bytes 364
  53.1 5.0 %collective-permute-start.12 = (bf16[1,8,16,128]{3,2,1,0:T(8,128)(2,1)S(1)}, bf16[1,8,16,128]{3,2,1,0:T(8,128)(2,1)S(1)}, u32[]{:S(2)}, u32[]{:S(2)}) collective-permute-start(bf16[1,8,16,128]{3,2,1,0:T(8,128)(2,1)S(1)} %get-tuple-element.39), channel_id=1, source_target_pairs={{0,4},{4,8},{8,12},{12,16},{16,20},{20,24},{24,28},{28,32},{32,36}... | collective-permute-start | bytes 98312 | tf_op jit(solution)/shard_map/ppermute | solution.py:19
  56.8 3.5 %collective-permute-start.13 = (bf16[1,8,16,128]{3,2,1,0:T(8,128)(2,1)S(1)}, bf16[1,8,16,128]{3,2,1,0:T(8,128)(2,1)S(1)}, u32[]{:S(2)}, u32[]{:S(2)}) collective-permute-start(bf16[1,8,16,128]{3,2,1,0:T(8,128)(2,1)S(1)} %get-tuple-element.40), channel_id=1, source_target_pairs={{4,0},{8,4},{12,8},{16,12},{20,16},{24,20},{28,24},{32,28},{36,32}... | collective-permute-start | bytes 98312 | tf_op jit(solution)/shard_map/ppermute | solution.py:20
  60.3 6.4 %collective-permute-start.14 = (bf16[4,1,16,128]{3,2,1,0:T(8,128)(2,1)S(1)}, bf16[4,1,16,128]{3,2,1,0:T(8,128)(2,1)S(1)}, u32[]{:S(2)}, u32[]{:S(2)}) collective-permute-start(bf16[4,1,16,128]{3,2,1,0:T(8,128)(2,1)S(1)} %get-tuple-element.27), channel_id=1, source_target_pairs={{1,0},{2,1},{3,2},{5,4},{6,5},{7,6},{9,8},{10,9},{11,10},{13,12},{... | collective-permute-start | bytes 49160 | tf_op jit(solution)/shard_map/ppermute | solution.py:20
  61.6 6.3 %collective-permute-start.15 = (bf16[4,1,16,128]{3,2,1,0:T(8,128)(2,1)S(1)}, bf16[4,1,16,128]{3,2,1,0:T(8,128)(2,1)S(1)}, u32[]{:S(2)}, u32[]{:S(2)}) collective-permute-start(bf16[4,1,16,128]{3,2,1,0:T(8,128)(2,1)S(1)} %get-tuple-element.28), channel_id=1, source_target_pairs={{0,1},{1,2},{2,3},{4,5},{5,6},{6,7},{8,9},{9,10},{10,11},{12,13},{... | collective-permute-start | bytes 49160 | tf_op jit(solution)/shard_map/ppermute | solution.py:19
